TPU v7x, 1024 devices: a whole 4x8x16 slice. The times are simulated.
1024 devices in a mesh: row: 8 (over y), col: 128 (over z, x, core).
Axes of the slice: x: 4, y: 8, z: 16, core: 2. Of those that a mesh axis runs over, the one named last changes fastest.
Arguments:
- left_tiles: bfloat16 [2, 64, 256, 256], P(None, 'row', 'col'), may hold values from 0.02 to 3, as said below
- right_tile_store: bfloat16 [512, 48, 256, 256], P('col', 'row'), may hold values from 0.019897461 to 1
- right_index: int32 [512, 48], P('col', 'row'), may hold values from 0 to 7, as said below
- right_count: int32 [512, 8], P('col', 'row'), may hold values from 1 to 6
Outputs:
- inflated: bfloat16 [2, 512, 256, 256], P(None, 'col', 'row')
Inputs may be any that keep to these rules, and one draw needn't show every extreme that they name: `right_index`: for each column block and each row index the 6 slots name distinct contraction blocks; only the first right_count of them are used. `left_tiles`: positive entries.
All inputs are finite; a program needn't handle non-finite values.
Results may differ from a plain program's by a relative error of at most 0.001.
Values may be sent and summed in bfloat16 or wider, within the bound.
A program may use at most 32 MiB of HBM per device.

v0:
```python
import jax
import jax.numpy as jnp
from jax import lax
from jax.sharding import Mesh
from jax.sharding import PartitionSpec as P

COL = ("col_0", "col_1", "col_2")


def in_order(parts, dim):
    lengths = list(parts.shape[1:])
    lengths[dim] *= parts.shape[0]
    return jnp.moveaxis(parts, 0, dim).reshape(lengths)


def all_blocks(value, axes, turns):
    parts = value
    for k in turns:
        parts = lax.all_gather(parts, axes[k])
    done = turns[::-1]
    back = [done.index(k) for k in range(len(axes))]
    parts = parts.transpose(*back, *range(len(axes), parts.ndim))
    return parts.reshape(-1, *value.shape)


def whole_of(value, axes, turns, dim):
    return in_order(all_blocks(value, axes, turns), dim)


def split_up(value, dim, size):
    before, after = (value.shape[:dim], value.shape[dim + 1 :])
    return jnp.moveaxis(value.reshape(*before, size, -1, *after), dim, 0)


def sent_and_summed(value, axis, dim):
    size = lax.axis_size(axis)
    parts = lax.all_to_all(split_up(value, dim, size), axis, 0, 0, tiled=True)
    return jnp.sum(parts, axis=0)


def from_everyone(value, axis):
    size = lax.axis_size(axis)
    return lax.all_to_all(
        jnp.broadcast_to(value[None], (size, *value.shape)), axis, 0, 0, tiled=True
    )


def of_everyone(value, axis):
    return from_everyone(value, axis).sum(axis=0)


def shards(left_tiles, right_tile_store, right_index, right_count):
    column_blocks = right_tile_store.shape[0]
    slot_total = right_tile_store.shape[1]
    window_blocks = left_tiles.shape[0]
    tile_size = right_tile_store.shape[2]
    live_mask = (jnp.arange(slot_total, dtype=jnp.int32)[None, :] < right_count).astype(
        jnp.bfloat16
    )
    flat_index = right_index.reshape(-1)
    shard_rows = whole_of(left_tiles, COL, (1, 0, 2), 2)
    picked = jnp.take(shard_rows, flat_index, axis=1)
    picked = picked.reshape(
        window_blocks, column_blocks, slot_total, shard_rows.shape[2], shard_rows.shape[3]
    )
    picked = picked * live_mask[None, :, :, None, None]
    partial_value = jnp.einsum(
        "ajqmb,jqbn->ajmn", picked, right_tile_store, preferred_element_type=jnp.float32
    )
    share = sent_and_summed(partial_value, "row", 2)
    squared = share * share
    column_sums = of_everyone(jnp.sum(squared, axis=(0, 2)), "row")
    scaled = squared * (window_blocks * tile_size / column_sums[None, :, None, :])
    return scaled.astype(jnp.bfloat16)


def solution(mesh):
    split = Mesh(
        mesh.devices.reshape(mesh.shape["row"], 16, 4, 2), ("row", "col_0", "col_1", "col_2")
    )
    return jax.shard_map(
        shards,
        mesh=split,
        in_specs=(
            P(None, "row", COL, None),
            P(COL, "row", None, None),
            P(COL, "row"),
            P(COL, "row"),
        ),
        out_specs=P(None, COL, "row", None),
        check_vma=False,
    )
```

profile of v0, /device:TPU:2, one launch (start us, length us, event | category | flops | bytes accessed | tf_op | source)
XLA Modules:
  0.0 218.4 jit_solution(2406194205319340908)
XLA Ops:
  6.5 0.0 copy-start
  6.5 0.0 all-gather.6.cloned.1.call-start
  6.5 0.9 copy.32
  7.4 22.7 %all-gather = bf16[8,8,2,256]{3,1,2,0:T(8,128)(2,1)} all-gather(bf16[2,8,2,256]{3,1,2,0:T(8,128)(2,1)S(1)} %copy.32), channel_id=2, replica_groups=mesh['row'=8,'col_0'=16,'col_1'=4,'col_2'=2] {'col_1'}, dimensions={0}, use_global_device_ids=true | all-gather | bytes 81920 | tf_op jit(solution)/shard_map/all_gather | solution.py:19
  30.1 0.0 all-gather.6.cloned.1.call-update
  30.1 0.0 all-gather.8.cloned.1.call-start
  30.1 72.1 %all-gather.6.cloned.1.call-done = bf16[64,2,8,2,256]{4,2,3,1,0:T(8,128)(2,1)} async-done(((bf16[4,2,8,2,256]{4,2,3,1,0:T(8,128)(2,1)}), bf16[64,2,8,2,256]{4,2,3,1,0:T(8,128)(2,1)}) %all-gather.6.cloned.1.call-update) | async-done | bytes 1048592 | tf_op jit(solution)/shard_map/all_gather | solution.py:19
  102.3 0.0 all-gather.8.cloned.1.call-update
  102.3 0.8 reshape.80
  103.1 0.8 fusion.3
  103.8 21.5 %all-gather.8.cloned.1.call-done = bf16[32,4,2,8,2,256]{5,3,4,2,1,0:T(8,128)(2,1)} async-done(((bf16[16,4,2,8,2,256]{5,3,4,2,1,0:T(8,128)(2,1)}), bf16[32,4,2,8,2,256]{5,3,4,2,1,0:T(8,128)(2,1)}) %all-gather.8.cloned.1.call-update) | async-done | bytes 2097168 | tf_op jit(solution)/shard_map/all_gather | solution.py:19
  125.3 1.8 copy.33
  127.1 0.2 copy.34
  127.3 1.8 copy.35
  129.1 6.0 %gather_fusion = bf16[24,2,256,256]{3,2,1,0:T(8,128)(2,1)} fusion(bf16[2,8,256,256]{3,2,1,0:T(8,128)(2,1)} %copy.35, s32[1024]{0:T(1024)S(1)} %pad_clamp_fusion), kind=kCustom, calls=%fused_computation | custom fusion | bytes 12583008 | tf_op jit(solution)/shard_map/jit(_take)/gather | solution.py:62
  135.1 3.2 %copy.36 = bf16[2,24,256,256]{3,2,1,0:T(8,128)(2,1)S(1)} copy(bf16[2,24,256,256]{3,2,0,1:T(8,128)(2,1)} %bitcast.28) | data formatting | bytes 12582912 | tf_op jit(solution)/shard_map/jit(_take)/gather | solution.py:62
  138.3 0.0 copy-done
  138.3 1.9 fusion
  140.2 0.1 copy.49
  140.4 58.3 %all_to_all.10 = f32[8,2,4,32,256]{4,3,1,2,0:T(8,128)} all-to-all(f32[8,2,4,32,256]{4,3,1,2,0:T(8,128)S(1)} %bitcast.31), channel_id=1, replica_groups=mesh['row'=8,'col_0'=16,'col_1'=4,'col_2'=2] {'row'}, dimensions={0} | all-to-all | bytes 4194304 | tf_op jit(solution)/shard_map/all_to_all | solution.py:37
  198.6 1.8 reduce_sum.27
  200.5 10.4 %all_to_all.11 = f32[8,4,256]{2,1,0:T(4,128)S(1)} all-to-all(f32[8,4,256]{2,1,0:T(4,128)S(1)} %broadcast_in_dim.21), channel_id=1, replica_groups=mesh['row'=8,'col_0'=16,'col_1'=4,'col_2'=2] {'row'}, dimensions={0} | all-to-all | bytes 65536 | tf_op jit(solution)/shard_map/all_to_all | solution.py:43
  210.9 0.7 copy.41
  (7 shorter events, 0.1 us)
Async XLA Ops:
  6.5 131.8 %copy-start = (bf16[4,6,256,256]{3,2,1,0:T(8,128)(2,1)S(1)}, bf16[4,6,256,256]{3,2,1,0:T(8,128)(2,1)}, u32[]{:S(2)}) copy-start(bf16[4,6,256,256]{3,2,1,0:T(8,128)(2,1)} %param.5) | copy-start | bytes 9437188
  6.5 95.7 %all-gather.6.cloned.1.call-start = ((), (), s32[]{:S(2)}) async-start(), calls=%async_computation.2 | async-start | bytes 1114112 | tf_op jit(solution)/shard_map/all_gather | solution.py:19
  30.1 95.2 %all-gather.8.cloned.1.call-start = ((), (), s32[]{:S(2)}) async-start(), calls=%async_computation.3 | async-start | bytes 3145728 | tf_op jit(solution)/shard_map/all_gather | solution.py:19
Sparse Core Ops, SparseCore 0:
  30.2 71.9 all-gather.5
  104.9 20.3 all-gather.7
where the time goes:
time: 219 us; the launch traced here: 218 us
  waiting for transfers between devices  93.6 us (43%)
  blocking collectives  91.3 us (42%)
  local copies, waits for them, and re-layouts  15.4 us (7%)
  between operations  13.5 us (6%)
  other arithmetic  2.64 us (1%)
    all_gather x2, waiting for transfers between devices, all_blocks(): parts = lax.all_gather(parts, axes[k])  93.6 us
    all_to_all x1, blocking collectives, sent_and_summed(): parts = lax.all_to_all(split_up(value, dim, size), axis, 0, 0, tiled=True)  58.3 us
    all_gather x1, blocking collectives, all_blocks(): parts = lax.all_gather(parts, axes[k])  22.7 us
    all_to_all x1, blocking collectives, from_everyone(): lax.all_to_all(jnp.broadcast_to(value[None], (size, *value.shape)), axis,...  10.4 us
    gather x2, local copies, waits for them, and re-layouts, shards(): picked = jnp.take(shard_rows, flat_index, axis=1)  9.2 us
  transfers between devices with their start and end apart: 2, of which 2 were waited for; matrix products, arithmetic and copies ran while one was open for 1% of the time, Pallas kernels for 0%

commit v1 on v0

v1 whole, which is shorter than its diff:
```python
import math

import jax
import jax.numpy as jnp
from jax import lax
from jax.experimental import pallas as pl
from jax.experimental.pallas import tpu as pltpu
from jax.sharding import Mesh
from jax.sharding import PartitionSpec as P

COL = ("col_0", "col_1", "col_2")
AXES = ("row", *COL)

Y, Z, X, C = 8, 16, 4, 2
REACH = 4
SLOTS_1 = 2 * REACH + 1
SLOTS_2 = Z - SLOTS_1

LOW, HIGH = math.log(0.1), math.log(40000.0)
CENTRE = (LOW + HIGH) / 2
STEP = (HIGH - LOW) / 65000


def encode(value):
    scaled = (jnp.log(value) - CENTRE) * (1 / STEP)
    return jnp.round(scaled).astype(jnp.int32).astype(jnp.int16)


def decode(code):
    return jnp.exp(code.astype(jnp.int32).astype(jnp.float32) * STEP + CENTRE)


def kernel(
    index_ref, count_ref, left_ref, right_hbm, out_ref,
    right, parts, rows, partial, sent, got, sums, sums_in,
    load_sem, z_sem, x_sem, core_sem, row_sem, sums_sem, send_sem,
):
    y, z, x, c = (lax.axis_index(name) for name in AXES)
    blocks, slots, edge = right_hbm.shape[0], right_hbm.shape[1], right_hbm.shape[2]
    window, kr = left_ref.shape[0], left_ref.shape[1]
    share = edge // Y
    piece = parts.shape[1]

    def at(dy=0, dz=0, dx=0, dc=0):
        return (
            lax.rem(y + dy + Y, Y),
            lax.rem(z + dz + Z, Z),
            lax.rem(x + dx + X, X),
            lax.rem(c + dc, C),
        )

    loads = [
        pltpu.make_async_copy(right_hbm.at[j], right.at[j], load_sem.at[j])
        for j in range(blocks)
    ]
    for load in loads:
        load.start()

    peers = [at(dz=d) for d in range(-REACH, REACH + 1) if d]
    peers += [at(dx=1), at(dx=-1), at(dc=1)]
    peers += [at(dy=d) for d in range(1, Y)]
    barrier = pltpu.get_barrier_semaphore()
    for peer in peers:
        pl.semaphore_signal(barrier, inc=1, device_id=peer, device_id_type=pl.DeviceIdType.MESH)

    def base(dx, dc=0):
        return (lax.rem(x + dx + X, X) * C + lax.rem(c + dc, C)) * Z

    mine = base(0)
    parts[mine + REACH] = left_ref[...].reshape(piece, edge)
    rows[:, kr] = jnp.zeros((window, edge, edge), jnp.bfloat16)
    pl.semaphore_wait(barrier, len(peers))

    def copy(src, dst, recv, to, kind=0):
        return pltpu.make_async_remote_copy(
            src_ref=src, dst_ref=dst, send_sem=send_sem.at[kind], recv_sem=recv,
            device_id=to, device_id_type=pl.DeviceIdType.MESH,
        )

    def pass_on(first, number, recv, to):
        where = parts.at[pl.ds(first, number)]
        copy(where, where, recv, to).start()

    def arrived(number, recv):
        where = parts.at[pl.ds(0, number)]
        pltpu.make_async_copy(where, where, recv).wait()

    own = parts.at[mine + REACH]
    for d in range(REACH, 0, -1):
        far = d == REACH
        copy(own, parts.at[mine + REACH - d], z_sem.at[0 if far else 2], at(dz=d)).start()
        copy(own, parts.at[mine + REACH + d], z_sem.at[1 if far else 2], at(dz=-d)).start()
    arrived(1, z_sem.at[0])
    for d in range(REACH, 0, -1):
        copy(parts.at[mine], parts.at[mine + Z - d], z_sem.at[3], at(dz=d)).start()
    arrived(1, z_sem.at[1])
    for d in range(REACH - 1, 0, -1):
        copy(
            parts.at[mine + 2 * REACH], parts.at[mine + 2 * REACH + d], z_sem.at[3], at(dz=-d)
        ).start()

    batches = ((0, SLOTS_1), (SLOTS_1, SLOTS_2))

    def to_core(b, way, dx):
        first, number = batches[b]
        pass_on(base(dx) + first, number, core_sem.at[b, way], at(dc=1))

    def near(b):
        first, number = batches[b]
        pass_on(mine + first, number, x_sem.at[b, 0], at(dx=1))
        pass_on(mine + first, number, x_sem.at[b, 1], at(dx=-1))
        to_core(b, 0, 0)

    def across(b):
        first, number = batches[b]
        half = number // 2
        arrived(number, x_sem.at[b, 0])
        pass_on(base(-1) + first, half, x_sem.at[b, 2], at(dx=1))
        arrived(number, x_sem.at[b, 1])
        pass_on(base(1) + first + half, number - half, x_sem.at[b, 3], at(dx=-1))
        to_core(b, 1, -1)
        to_core(b, 2, 1)

    def last(b):
        first, number = batches[b]
        half = number // 2
        arrived(half, x_sem.at[b, 2])
        arrived(number - half, x_sem.at[b, 3])
        to_core(b, 3, 2)

    out_row = lax.broadcasted_iota(jnp.int32, (edge, edge), 0)
    in_row = lax.broadcasted_iota(jnp.int32, (edge, edge), 1)
    per = piece // (window * kr)
    span = per * X * C
    tile, within = lax.div(out_row, span), lax.rem(out_row, span)
    source = lax.div(within, per) * piece + tile * per + lax.rem(within, per)
    order = (source == in_row).astype(jnp.float32).astype(jnp.bfloat16)

    def spread(b):
        first, number = batches[b]
        for way in range(4):
            arrived(number, core_sem.at[b, way])

        def one(slot, carry):
            mixed = jnp.concatenate([parts[d * Z + slot] for d in range(X * C)], axis=0)
            placed = jnp.dot(order, mixed, preferred_element_type=jnp.float32)
            placed = placed.astype(jnp.bfloat16).reshape(window, kr, span, edge)
            start = pl.multiple_of(lax.rem(z + slot + Z - REACH, Z) * span, span)
            rows[:, pl.ds(0, kr), pl.ds(start, span), :] = placed
            return carry

        lax.fori_loop(first, first + number, one, 0)

    arrived(2 * REACH - 2, z_sem.at[2])
    near(0)
    across(0)
    arrived(SLOTS_2, z_sem.at[3])
    near(1)
    last(0)
    across(1)
    spread(0)
    last(1)
    for load in loads:
        load.wait()
    spread(1)

    def multiply(slot, dy):
        start = pl.multiple_of(lax.rem(y + dy + Y, Y) * share, share)

        def one(j, carry):
            live = count_ref[j, 0]
            picked = []
            for q in range(slots):
                k = jnp.where(q < live, index_ref[j, q], kr)
                picked.append(rows[:, k, pl.ds(start, share), :].reshape(window * share, edge))
            partial[slot, j] = jnp.dot(
                jnp.concatenate(picked, axis=1),
                right[j].reshape(slots * edge, edge),
                preferred_element_type=jnp.float32,
            )
            return carry

        lax.fori_loop(0, blocks, one, 0)

    half = blocks // 2
    far = Y // 2

    def message(step, way, j):
        return (step * 2 + way) * blocks + j

    def pass_sum(step, way, j, add):
        slot = 0 if step == 0 else way
        value = partial[slot, j]
        if add:
            wait_sum(step - 1, way, j)
            value = value + decode(got[message(step - 1, way, j)])
        n = message(step, way, j)
        place = n - (way if step == 0 else 1) * blocks
        sent[place] = encode(value)
        copy(sent.at[place], got.at[n], row_sem.at[n], at(dy=1 if way == 0 else -1), 1).start()

    def wait_sum(step, way, j):
        n = message(step, way, j)
        pltpu.make_async_copy(got.at[n], got.at[n], row_sem.at[n]).wait()

    def each(first, last_one, body):
        def one(j, carry):
            body(j)
            return carry

        lax.fori_loop(first, last_one, one, 0)

    multiply(0, far)
    each(0, half, lambda j: pass_sum(0, 0, j, False))
    each(half, blocks, lambda j: pass_sum(0, 1, j, False))
    for step in range(1, far):
        multiply(0, far - step)
        multiply(1, step - far)
        if step == 1:
            each(half, blocks, lambda j: pass_sum(1, 0, j, False))
            each(0, half, lambda j: pass_sum(1, 1, j, False))
            each(0, half, lambda j: pass_sum(1, 0, j, True))
            each(half, blocks, lambda j: pass_sum(1, 1, j, True))
        else:
            def both(j, step=step):
                pass_sum(step, 0, j, True)
                pass_sum(step, 1, j, True)

            each(0, blocks, both)
    multiply(0, 0)
    for j in range(blocks):
        wait_sum(far - 1, 0, j)
        wait_sum(far - 1, 1, j)
        product = (
            partial[0, j]
            + decode(got[message(far - 1, 0, j)])
            + decode(got[message(far - 1, 1, j)])
        )
        squared = product * product
        partial[1, j] = squared
        sums[j : j + 1, :] = jnp.sum(squared, axis=0, keepdims=True)
    for d in range(1, Y):
        copy(sums, sums_in.at[d - 1], sums_sem.at[0], at(dy=d), 2).start()
    pltpu.make_async_copy(sums_in, sums_in, sums_sem.at[0]).wait()
    total = sums[...]
    for d in range(Y - 1):
        total = total + sums_in[d]
    scale = (window * edge) / total
    for j in range(blocks):
        scaled = partial[1, j] * scale[j : j + 1, :]
        out_ref[:, j] = scaled.astype(jnp.bfloat16).reshape(window, share, edge)

    for kind, whole in enumerate((parts.at[pl.ds(0, X * C * Z - 1)], sent, sums_in)):
        pltpu.make_async_copy(whole, whole, send_sem.at[kind]).wait()


def shards(left_tiles, right_tile_store, right_index, right_count):
    window, kr, per, edge = left_tiles.shape
    blocks, slots = right_tile_store.shape[:2]
    share = edge // Y
    piece = window * kr * per
    messages = (Y // 2) * 2 * blocks
    return pl.pallas_call(
        kernel,
        out_shape=jax.ShapeDtypeStruct((window, blocks, share, edge), jnp.bfloat16),
        in_specs=[
            pl.BlockSpec(memory_space=pltpu.SMEM),
            pl.BlockSpec(memory_space=pltpu.SMEM),
            pl.BlockSpec(memory_space=pltpu.VMEM),
            pl.BlockSpec(memory_space=pl.ANY),
        ],
        out_specs=pl.BlockSpec(memory_space=pltpu.VMEM),
        scratch_shapes=[
            pltpu.VMEM((blocks, slots, edge, edge), jnp.bfloat16),
            pltpu.VMEM((X * C * Z, piece, edge), jnp.bfloat16),
            pltpu.VMEM((window, kr + 1, edge, edge), jnp.bfloat16),
            pltpu.VMEM((2, blocks, window * share, edge), jnp.float32),
            pltpu.VMEM((messages - blocks, window * share, edge), jnp.int16),
            pltpu.VMEM((messages, window * share, edge), jnp.int16),
            pltpu.VMEM((blocks, edge), jnp.float32),
            pltpu.VMEM((Y - 1, blocks, edge), jnp.float32),
            pltpu.SemaphoreType.DMA((blocks,)),
            pltpu.SemaphoreType.DMA((4,)),
            pltpu.SemaphoreType.DMA((2, 4)),
            pltpu.SemaphoreType.DMA((2, 4)),
            pltpu.SemaphoreType.DMA((messages,)),
            pltpu.SemaphoreType.DMA((1,)),
            pltpu.SemaphoreType.DMA((3,)),
        ],
        compiler_params=pltpu.CompilerParams(
            collective_id=0, has_side_effects=True, vmem_limit_bytes=48 * 1024 * 1024
        ),
    )(right_index, right_count, left_tiles, right_tile_store)


def solution(mesh):
    split = Mesh(mesh.devices.reshape(Y, Z, X, C), AXES)
    return jax.shard_map(
        shards,
        mesh=split,
        in_specs=(
            P(None, "row", COL, None),
            P(COL, "row", None, None),
            P(COL, "row"),
            P(COL, "row"),
        ),
        out_specs=P(None, COL, "row", None),
        check_vma=False,
    )
```

time: 219 us -> 71.4 us (0.33)
  the two profiles are of different devices: /device:TPU:2 before, /device:TPU:4 now
where the time goes in v1:
time: 71.4 us; the launch traced here: 71.1 us
  Pallas kernels  66.4 us (93%)
  local copies, waits for them, and re-layouts  4.69 us (7%)
    pallas_call x1, Pallas kernels, shards(): pl.pallas_call(kernel, out_shape=jax.ShapeDtypeStruct((window, blocks, sh...  66.4 us
    unnamed x8, local copies, waits for them, and re-layouts  4.69 us

profile of v1, /device:TPU:4, one launch (start us, length us, event | category | flops | bytes accessed | tf_op | source)
XLA Modules:
  0.0 71.1 jit_solution(10999187254880288055)
XLA Ops:
  0.0 0.7 %copy.5.count_ref = s32[4,1]{1,0:T(4,128)S(1)} copy(s32[4,1]{0,1:T(1,128)} %param.7) | data formatting | bytes 32 | tf_op args[3]
  0.7 0.0 copy-start
  0.7 1.9 %copy-done = bf16[4,6,256,256]{3,2,1,0:T(8,128)(2,1)S(1)} copy-done((bf16[4,6,256,256]{3,2,1,0:T(8,128)(2,1)S(1)}, bf16[4,6,256,256]{3,2,1,0:T(8,128)(2,1)}, u32[]{:S(2)}) %copy-start) | copy-done | bytes 3145752
  2.6 0.0 copy-start.1
  2.6 0.7 %copy-done.1 = bf16[2,8,2,256]{3,2,1,0:T(2,128)(2,1)S(1)} copy-done((bf16[2,8,2,256]{3,2,1,0:T(2,128)(2,1)S(1)}, bf16[2,8,2,256]{3,2,1,0:T(2,128)(2,1)}, u32[]{:S(2)}) %copy-start.1) | copy-done | bytes 16408
  3.3 0.0 copy-start.2
  3.4 0.7 copy-done.2
  4.0 66.4 %shard_map.46 = bf16[2,4,32,256]{3,2,1,0:T(8,128)(2,1)S(1)} custom-call(s32[4,6]{1,0:T(4,128)S(1)} %copy-done.2, s32[4,1]{1,0:T(4,128)S(1)} %copy.5.count_ref, bf16[2,8,2,256]{3,2,1,0:T(2,128)(2,1)S(1)} %copy-done.1, bf16[4,6,256,256]{3,2,1,0:T(8,128)(2,1)S(1)} %copy-done), custom_call_target="tpu_custom_call" | custom-call | tf_op jit(solution)/shard_map/pallas_call | solution.py:263
  70.4 0.7 copy.7
Async XLA Ops:
  0.7 1.9 %copy-start = (bf16[4,6,256,256]{3,2,1,0:T(8,128)(2,1)S(1)}, bf16[4,6,256,256]{3,2,1,0:T(8,128)(2,1)}, u32[]{:S(2)}) copy-start(bf16[4,6,256,256]{3,2,1,0:T(8,128)(2,1)} %right_hbm.1) | copy-start | bytes 9437188
  2.6 0.7 %copy-start.1 = (bf16[2,8,2,256]{3,2,1,0:T(2,128)(2,1)S(1)}, bf16[2,8,2,256]{3,2,1,0:T(2,128)(2,1)}, u32[]{:S(2)}) copy-start(bf16[2,8,2,256]{3,2,1,0:T(2,128)(2,1)} %left_ref.1) | copy-start | bytes 49156
  3.3 0.7 copy-start.2

commit v2 on v1

v2 whole, which is shorter than its diff:
```python
import math

import jax
import jax.numpy as jnp
from jax import lax
from jax.experimental import pallas as pl
from jax.experimental.pallas import tpu as pltpu
from jax.sharding import Mesh
from jax.sharding import PartitionSpec as P

COL = ("col_0", "col_1", "col_2")
AXES = ("row", *COL)

Y, Z, X, C = 8, 16, 4, 2
REACH = 4
SLOTS_1 = 2 * REACH + 1
SLOTS_2 = Z - SLOTS_1

LOW, HIGH = math.log(0.1), math.log(40000.0)
CENTRE = (LOW + HIGH) / 2
STEP = (HIGH - LOW) / 65000


def encode(value):
    scaled = (jnp.log(value) - CENTRE) * (1 / STEP)
    return jnp.round(scaled).astype(jnp.int32).astype(jnp.int16)


def decode(code):
    return jnp.exp(code.astype(jnp.int32).astype(jnp.float32) * STEP + CENTRE)


def kernel(
    index_hbm, count_hbm, left_hbm, right_hbm, out_ref,
    index_ref, count_ref, left_ref, right, parts, rows, partial, sent, got, sums, sums_in,
    load_sem, small_sem, z_sem, x_sem, core_sem, row_sem, sums_sem, send_sem,
):
    y, z, x, c = (lax.axis_index(name) for name in AXES)
    blocks, slots, edge = right_hbm.shape[0], right_hbm.shape[1], right_hbm.shape[2]
    window, kr = left_ref.shape[0], left_ref.shape[1]
    share = edge // Y
    piece = parts.shape[2]

    def at(dy=0, dz=0, dx=0, dc=0):
        return (
            lax.rem(y + dy + Y, Y),
            lax.rem(z + dz + Z, Z),
            lax.rem(x + dx + X, X),
            lax.rem(c + dc, C),
        )

    loads = [
        pltpu.make_async_copy(right_hbm.at[j], right.at[j], load_sem.at[j])
        for j in range(blocks)
    ]
    small = [
        pltpu.make_async_copy(src, dst, small_sem.at[n])
        for n, (src, dst) in enumerate(
            ((left_hbm, left_ref), (index_hbm, index_ref), (count_hbm, count_ref))
        )
    ]
    for load in small + loads:
        load.start()

    peers = [at(dz=d) for d in range(-REACH, REACH + 1) if d]
    peers += [at(dx=1), at(dx=-1), at(dc=1)]
    peers += [at(dy=d) for d in range(1, Y)]
    barrier = pltpu.get_barrier_semaphore()
    for peer in peers:
        pl.semaphore_signal(barrier, inc=1, device_id=peer, device_id_type=pl.DeviceIdType.MESH)

    def base(dx, dc=0):
        return (lax.rem(x + dx + X, X) * C + lax.rem(c + dc, C)) * Z

    mine = base(0)
    small[0].wait()
    for w in range(window):
        parts[w, mine + REACH] = left_ref[w].reshape(piece, edge)
    rows[:, kr] = jnp.zeros((window, edge, edge), jnp.bfloat16)

    per = piece // kr
    span = per * X * C
    out_row = lax.broadcasted_iota(jnp.int32, (kr * span, kr * span), 0)
    in_row = lax.broadcasted_iota(jnp.int32, (kr * span, kr * span), 1)
    tile, within = lax.div(out_row, span), lax.rem(out_row, span)
    source = lax.div(within, per) * piece + tile * per + lax.rem(within, per)
    order = (source == in_row).astype(jnp.float32).astype(jnp.bfloat16)
    pl.semaphore_wait(barrier, len(peers))

    def copy(src, dst, recv, to, kind):
        return pltpu.make_async_remote_copy(
            src_ref=src, dst_ref=dst, send_sem=send_sem.at[kind], recv_sem=recv,
            device_id=to, device_id_type=pl.DeviceIdType.MESH,
        )

    def pass_on(w, first, number, recv, to):
        where = parts.at[w, pl.ds(first, number)]
        copy(where, where, recv, to, w).start()

    def arrived(number, recv):
        where = parts.at[0, pl.ds(0, number)]
        pltpu.make_async_copy(where, where, recv).wait()

    def start_z(w):
        own = parts.at[w, mine + REACH]
        for d in range(REACH, 0, -1):
            far = d == REACH
            up = parts.at[w, mine + REACH - d]
            down = parts.at[w, mine + REACH + d]
            copy(own, up, z_sem.at[w, 0 if far else 2], at(dz=d), w).start()
            copy(own, down, z_sem.at[w, 1 if far else 2], at(dz=-d), w).start()

    def relay_z(w):
        low, high = parts.at[w, mine], parts.at[w, mine + 2 * REACH]
        arrived(1, z_sem.at[w, 0])
        for d in range(REACH, 0, -1):
            copy(low, parts.at[w, mine + Z - d], z_sem.at[w, 3], at(dz=d), w).start()
        arrived(1, z_sem.at[w, 1])
        for d in range(REACH - 1, 0, -1):
            to = parts.at[w, mine + 2 * REACH + d]
            copy(high, to, z_sem.at[w, 3], at(dz=-d), w).start()

    batches = ((0, SLOTS_1), (SLOTS_1, SLOTS_2))

    def to_core(w, b, way, dx):
        first, number = batches[b]
        pass_on(w, base(dx) + first, number, core_sem.at[w, b, way], at(dc=1))

    def near(w, b):
        first, number = batches[b]
        arrived(2 * REACH - 2 if b == 0 else SLOTS_2, z_sem.at[w, 2 + b])
        pass_on(w, mine + first, number, x_sem.at[w, b, 0], at(dx=1))
        pass_on(w, mine + first, number, x_sem.at[w, b, 1], at(dx=-1))
        to_core(w, b, 0, 0)

    def across(w, b):
        first, number = batches[b]
        half = number // 2
        arrived(number, x_sem.at[w, b, 0])
        pass_on(w, base(-1) + first, half, x_sem.at[w, b, 2], at(dx=1))
        arrived(number, x_sem.at[w, b, 1])
        pass_on(w, base(1) + first + half, number - half, x_sem.at[w, b, 3], at(dx=-1))
        to_core(w, b, 1, -1)
        to_core(w, b, 2, 1)

    def last(w, b):
        first, number = batches[b]
        half = number // 2
        arrived(half, x_sem.at[w, b, 2])
        arrived(number - half, x_sem.at[w, b, 3])
        to_core(w, b, 3, 2)

    def spread(w, b):
        first, number = batches[b]
        for way in range(4):
            arrived(number, core_sem.at[w, b, way])

        def one(slot, carry):
            mixed = jnp.concatenate([parts[w, d * Z + slot] for d in range(X * C)], axis=0)
            placed = jnp.dot(order, mixed, preferred_element_type=jnp.float32)
            placed = placed.astype(jnp.bfloat16).reshape(kr, span, edge)
            start = pl.multiple_of(lax.rem(z + slot + Z - REACH, Z) * span, span)
            rows[w, pl.ds(0, kr), pl.ds(start, span), :] = placed
            return carry

        lax.fori_loop(first, first + number, one, 0)

    half = blocks // 2
    far = Y // 2

    def each(first, last_one, body):
        def one(j, carry):
            body(j)
            return carry

        lax.fori_loop(first, last_one, one, 0)

    def multiply(w, *targets):
        starts = [pl.multiple_of(lax.rem(y + dy + Y, Y) * share, share) for dy in targets]

        def one(j):
            live = count_ref[0, j]
            picked = []
            for q in range(slots):
                k = jnp.where(q < live, index_ref[j, q], kr)
                picked.append(
                    jnp.concatenate([rows[w, k, pl.ds(at, share), :] for at in starts], axis=0)
                )
            result = jnp.dot(
                jnp.concatenate(picked, axis=1),
                right[j].reshape(slots * edge, edge),
                preferred_element_type=jnp.float32,
            )
            for slot in range(len(starts)):
                partial[w, slot, j] = result[slot * share : (slot + 1) * share]

        each(0, blocks, one)

    def message(step, way, j):
        return (step * 2 + way) * blocks + j

    def wait_sum(w, step, way, j):
        n = message(step, way, j)
        pltpu.make_async_copy(got.at[w, n], got.at[w, n], row_sem.at[w, n]).wait()

    def pass_sum(w, step, way, j, add):
        value = partial[w, 0 if step == 0 else way, j]
        if add:
            wait_sum(w, step - 1, way, j)
            value = value + decode(got[w, message(step - 1, way, j)])
        n = message(step, way, j)
        place = n - (way if step == 0 else 1) * blocks
        sent[w, place] = encode(value)
        to = at(dy=1 if way == 0 else -1)
        copy(sent.at[w, place], got.at[w, n], row_sem.at[w, n], to, 2).start()

    def first_sums(w):
        multiply(w, far)
        each(0, half, lambda j: pass_sum(w, 0, 0, j, False))
        each(half, blocks, lambda j: pass_sum(w, 0, 1, j, False))

    def second_sums(w):
        multiply(w, far - 1, 1 - far)
        each(half, blocks, lambda j: pass_sum(w, 1, 0, j, False))
        each(0, half, lambda j: pass_sum(w, 1, 1, j, False))

    def next_sums(w, step):
        if step == 1:
            def both(j):
                pass_sum(w, 1, 0, j, True)
                pass_sum(w, 1, 1, j + half, True)

            each(0, half, both)
        else:
            def both(j):
                pass_sum(w, step, 0, j, True)
                pass_sum(w, step, 1, j, True)

            each(0, blocks, both)
        left = far - step - 1
        multiply(w, *((left, -left) if left else (0,)))

    for w in range(window):
        start_z(w)
    for w in range(window):
        relay_z(w)
    for w in range(window):
        near(w, 0)
    for load in small[1:] + loads:
        load.wait()
    for w in range(window):
        across(w, 0)
    for w in range(window):
        near(w, 1)
    for w in range(window):
        last(w, 0)
    spread(0, 0)
    across(0, 1)
    spread(1, 0)
    across(1, 1)
    last(0, 1)
    last(1, 1)
    spread(0, 1)
    first_sums(0)
    spread(1, 1)
    first_sums(1)
    for w in range(window):
        second_sums(w)
    for step in range(1, far):
        for w in range(window):
            next_sums(w, step)

    for w in range(window):
        for j in range(blocks):
            wait_sum(w, far - 1, 0, j)
            wait_sum(w, far - 1, 1, j)
            product = (
                partial[w, 0, j]
                + decode(got[w, message(far - 1, 0, j)])
                + decode(got[w, message(far - 1, 1, j)])
            )
            squared = product * product
            partial[w, 1, j] = squared
            column = jnp.sum(squared, axis=0, keepdims=True)
            sums[j : j + 1, :] = column if w == 0 else sums[j : j + 1, :] + column
    for d in range(1, Y):
        copy(sums, sums_in.at[d - 1], sums_sem.at[0], at(dy=d), 3).start()
    pltpu.make_async_copy(sums_in, sums_in, sums_sem.at[0]).wait()
    total = sums[...]
    for d in range(Y - 1):
        total = total + sums_in[d]
    scale = (window * edge) / total
    for j in range(blocks):
        for w in range(window):
            out_ref[w, j] = (partial[w, 1, j] * scale[j : j + 1, :]).astype(jnp.bfloat16)

    for w in range(window):
        moved = parts.at[w, pl.ds(0, X * C * Z - 1)]
        pltpu.make_async_copy(moved, moved, send_sem.at[w]).wait()
    pltpu.make_async_copy(sent, sent, send_sem.at[2]).wait()
    pltpu.make_async_copy(sums_in, sums_in, send_sem.at[3]).wait()


def shards(left_tiles, right_tile_store, right_index, right_count):
    window, kr, per, edge = left_tiles.shape
    blocks, slots = right_tile_store.shape[:2]
    share = edge // Y
    piece = kr * per
    messages = (Y // 2) * 2 * blocks
    return pl.pallas_call(
        kernel,
        out_shape=jax.ShapeDtypeStruct((window, blocks, share, edge), jnp.bfloat16),
        in_specs=[
            pl.BlockSpec(memory_space=pltpu.HBM),
            pl.BlockSpec(memory_space=pltpu.HBM),
            pl.BlockSpec(memory_space=pltpu.HBM),
            pl.BlockSpec(memory_space=pltpu.HBM),
        ],
        out_specs=pl.BlockSpec(memory_space=pltpu.VMEM),
        scratch_shapes=[
            pltpu.SMEM((blocks, slots), jnp.int32),
            pltpu.SMEM((1, blocks), jnp.int32),
            pltpu.VMEM((window, kr, per, edge), jnp.bfloat16),
            pltpu.VMEM((blocks, slots, edge, edge), jnp.bfloat16),
            pltpu.VMEM((window, X * C * Z, piece, edge), jnp.bfloat16),
            pltpu.VMEM((window, kr + 1, edge, edge), jnp.bfloat16),
            pltpu.VMEM((window, 2, blocks, share, edge), jnp.float32),
            pltpu.VMEM((window, messages - blocks, share, edge), jnp.int16),
            pltpu.VMEM((window, messages, share, edge), jnp.int16),
            pltpu.VMEM((blocks, edge), jnp.float32),
            pltpu.VMEM((Y - 1, blocks, edge), jnp.float32),
            pltpu.SemaphoreType.DMA((blocks,)),
            pltpu.SemaphoreType.DMA((3,)),
            pltpu.SemaphoreType.DMA((window, 4)),
            pltpu.SemaphoreType.DMA((window, 2, 4)),
            pltpu.SemaphoreType.DMA((window, 2, 4)),
            pltpu.SemaphoreType.DMA((window, messages)),
            pltpu.SemaphoreType.DMA((1,)),
            pltpu.SemaphoreType.DMA((4,)),
        ],
        compiler_params=pltpu.CompilerParams(
            collective_id=0, has_side_effects=True, vmem_limit_bytes=67_043_328
        ),
    )(right_index, right_count.T, left_tiles, right_tile_store)


def solution(mesh):
    split = Mesh(mesh.devices.reshape(Y, Z, X, C), AXES)
    return jax.shard_map(
        shards,
        mesh=split,
        in_specs=(
            P(None, "row", COL, None),
            P(COL, "row", None, None),
            P(COL, "row"),
            P(COL, "row"),
        ),
        out_specs=P(None, COL, "row", None),
        check_vma=False,
    )
```

time: 71.4 us -> 68.9 us (0.965)
  the two profiles are of different devices: /device:TPU:4 before, /device:TPU:8 now
where the time goes in v2:
time: 68.9 us; the launch traced here: 68.7 us
  Pallas kernels  67.1 us (97%)
  local copies, waits for them, and re-layouts  1.57 us (2%)
    pallas_call x1, Pallas kernels, shards(): pl.pallas_call(kernel, out_shape=jax.ShapeDtypeStruct((window, blocks, sh...  67.1 us
    unnamed x1, local copies, waits for them, and re-layouts  1.57 us

profile of v2, /device:TPU:8, one launch (start us, length us, event | category | flops | bytes accessed | tf_op | source)
XLA Modules:
  0.0 68.7 jit_solution(12606259331692971243)
XLA Ops:
  0.0 67.1 %shard_map.46 = bf16[2,4,32,256]{3,2,1,0:T(8,128)(2,1)} custom-call(s32[4,6]{1,0:T(4,128)} %index_hbm.1, s32[1,4]{1,0:T(1,128)} %bitcast.1, bf16[2,8,2,256]{3,2,1,0:T(2,128)(2,1)} %left_hbm.1, bf16[4,6,256,256]{3,2,1,0:T(8,128)(2,1)} %right_hbm.1), custom_call_target="tpu_custom_call" | custom-call | tf_op jit(solution)/shard_map/pallas_call | solution.py:310
  67.1 1.6 %copy.6 = bf16[2,4,32,256]{3,2,1,0:T(8,128)(2,1)} copy(bf16[2,4,32,256]{3,2,1,0:T(8,128)(2,1)} %shard_map.46) | data formatting | bytes 262144
